TPU v7x, 32 devices: a whole 2x2x4 slice. The times are simulated.
32 devices in a mesh: seq: 16 (over z, y, core), head: 2 (over x).
Axes of the slice: x: 2, y: 2, z: 4, core: 2. Of those that a mesh axis runs over, the one named last changes fastest.
Arguments:
- tokens: bfloat16 [1, 8192, 2048], P(None, 'seq'), may hold values from -6 to 6
- qkv_weight: bfloat16 [2048, 3, 2048], P(None, None, 'head'), may hold values from -1 to 1
- persistent: bfloat16 [2, 128, 2048], P(None, None, 'head'), may hold values from -60 to 60
- rate_weight: float32 [2048], replicated, may hold values from -0.25 to 0.25
- forget_rate: float32 [1, 8192], P(None, 'seq'), may hold values from 9.765625e-07 to 0.0009765625
- momentum_decay: float32 [1], replicated, may hold values from 0.5 to 0.95
- forget_share: float32 [1], replicated, may hold values from 0.05 to 0.5
- memory: float32 [2048, 2, 4096], P('seq', None, 'head'), may hold values from -0.125 to 0.125
- momentum: float32 [2048, 2, 4096], P('seq', None, 'head'), may hold values from -0.0625 to 0.0625
Outputs:
- attended: bfloat16 [1, 8192, 2048], P(None, 'seq', 'head')
- memory_out: float32 [2048, 2, 4096], P('seq', None, 'head')
- momentum_out: float32 [2048, 2, 4096], P('seq', None, 'head')
All inputs are finite; a program needn't handle non-finite values.
Results may differ from a plain program's by a relative error of at most 0.01.
Values may be sent and summed in bfloat16 or wider, within the bound.
A program may use at most 128 MiB of HBM per device.

v0:
```python
import functools

import jax
import jax.numpy as jnp
from jax import lax
from jax.experimental import pallas as pl
from jax.experimental.pallas import tpu as pltpu
from jax.sharding import PartitionSpec as P

HEAD_DIM = 128
MESH = pl.DeviceIdType.MESH
VMEM_LIMIT = 67043328
F32, BF16 = jnp.float32, jnp.bfloat16


def remote(src, dst, send_sem, recv_sem, where):
    return pltpu.make_async_remote_copy(
        src_ref=src,
        dst_ref=dst,
        send_sem=send_sem,
        recv_sem=recv_sem,
        device_id=where,
        device_id_type=MESH,
    )


def dot(a, b):
    return jnp.dot(a, b, preferred_element_type=F32)


def dot_nt(a, b):
    return lax.dot_general(a, b, (((1,), (1,)), ((), ())), preferred_element_type=F32)


def dot_tn(a, b):
    return lax.dot_general(a, b, (((0,), (0,)), ((), ())), preferred_element_type=F32)


class Place:
    def __init__(self, n_seq, n_head):
        self.n_seq, self.n_head = n_seq, n_head
        self.length = n_seq // 4
        self.seq, self.head = lax.axis_index("seq"), lax.axis_index("head")
        self.line = self.seq // 4
        self.side = (self.seq // 2) % 2
        self.core = self.seq % 2

    def at(self, line, side, core):
        return {"seq": (line * 2 + side) * 2 + core}

    def order(self, i):
        left, right = self.line, self.length - 1 - self.line
        both = jnp.minimum(left, right)
        paired = i <= 2 * both
        step = jnp.where(paired, (i + 1) // 2, i - both)
        to_left = jnp.where(paired, i % 2 == 1, left > right)
        return jnp.where(to_left, self.line - step, self.line + step)

    def peers(self):
        return [{"head": (self.head + by) % self.n_head} for by in range(1, self.n_head)]


def rows_loop(total, step, body):
    @pl.loop(0, total // step)
    def _(i):
        body(pl.ds(pl.multiple_of(i * step, step), step))


def forward_kernel(
    n_seq, n_head, lr_scale,
    tok, qkv, own, rate_w, forget,
    xx_out, yy_out, q_out, v_out, recall_out,
    W, wbuf, keys, query, values, zk, zz, hk, hq, wh, errs, err, recall, weight, frb,
    w_send, w_recv, f_send, f_recv, k_send, k_recv, e_send, e_recv, qkv_sem, out_sem,
):
    me = Place(n_seq, n_head)
    L, line, side, core, head = me.length, me.line, me.side, me.core, me.head
    chips = n_seq // 2
    count, width = tok.shape
    R, H = own.shape[1], own.shape[2]
    wide = 2 * R
    FB = values.shape[0]
    base = head * FB
    peers = me.peers()

    loads = [pltpu.make_async_copy(qkv.at[k], wbuf.at[s], qkv_sem.at[k]) for k, s in ((1, 0), (0, 1), (2, 0))]
    loads[0].start()
    loads[1].start()

    barrier = pltpu.get_barrier_semaphore()
    for by in range(1, n_seq):
        pl.semaphore_signal(barrier, inc=1, device_id={"seq": (me.seq + by) % n_seq}, device_id_type=MESH)
    for peer in peers:
        pl.semaphore_signal(barrier, inc=1, device_id=peer, device_id_type=MESH)
    pl.semaphore_wait(barrier, n_seq - 1 + n_head - 1)

    def block(w, l, m, c):
        return W.at[w, l * 2 + m, pl.ds(pl.multiple_of(c * R, R), R), :]

    def copy(w, l, m, c, way, src=None):
        where = (
            me.at(line + 1, side, core),
            me.at(line - 1, side, core),
            me.at(line, 1 - side, core),
            me.at(line, side, 1 - core),
        )[way]
        dst = block(w, l, m, c)
        chip = l * 2 + m
        return remote(dst if src is None else src, dst, w_send.at[w, way, chip], w_recv.at[w, chip * 2 + c], where)

    def spread(w, l, src, act):
        @pl.when((l <= line) & (line < L - 1))
        def _():
            act(copy(w, l, side, core, 0, src))

        @pl.when((l >= line) & (line > 0))
        def _():
            act(copy(w, l, side, core, 1, src))

        act(copy(w, l, side, core, 2, src))
        act(copy(w, l, side, core, 3, src))

    def start_own(w):
        spread(w, line, own.at[w], lambda c: c.start())
        W[w, line * 2 + side, pl.ds(pl.multiple_of(core * R, R), R), :] = own[w]

    def arrived(w, l, m, c):
        copy(w, l, m, c, 2).wait_recv()

    start_own(0)
    fcopies = []
    for by in range(1, n_seq):
        fcopies.append(
            remote(forget, frb.at[me.seq], f_send.at[by], f_recv.at[me.seq], {"seq": (me.seq + by) % n_seq})
        )
    for c in fcopies:
        c.start()
    frb[me.seq] = forget[...]

    def xcopy(which, buf, b, p):
        return remote(
            buf.at[base + b], buf.at[base + b], k_send.at[which, p, b], k_recv.at[which, base + b], peers[p]
        )

    def project(slot, b):
        cols = pl.ds(pl.multiple_of(b * wide, wide), wide)
        return dot(tok[...], wbuf[slot, :, cols]).astype(BF16)

    for which, (buf, slot) in enumerate(((keys, 0), (query, 1))):
        loads[which].wait()

        @pl.loop(0, FB)
        def _(b):
            buf[base + b] = project(slot, b)
            for p in range(n_head - 1):
                xcopy(which, buf, b, p).start()

        if which == 0:
            loads[2].start()
    loads[2].wait()

    @pl.loop(0, FB)
    def _(b):
        values[b] = project(0, b)

    for by in range(1, n_seq):
        other = (me.seq + by) % n_seq
        remote(forget, frb.at[other], f_send.at[by], f_recv.at[other], {"seq": other}).wait_recv()
    totals = jnp.sum(frb[...], axis=2, keepdims=True)
    which_seq = lax.broadcasted_iota(jnp.int32, totals.shape, 0)
    later = jnp.sum(jnp.where(which_seq > me.seq, totals, 0.0), axis=(0, 1, 2), keepdims=True)[0]

    def weigh(rows, start):
        x = tok[rows, :].astype(F32)
        rate = jnp.sum(x * rate_w[...], axis=1, keepdims=True)
        n = x.shape[0]
        t = lax.broadcasted_iota(jnp.int32, (n, count), 0) + start
        u = lax.broadcasted_iota(jnp.int32, (n, count), 1)
        tail = jnp.sum(jnp.where(u > t, forget[...], 0.0), axis=1, keepdims=True) + later
        weight[rows, :] = lr_scale * jax.nn.sigmoid(rate) * jnp.exp(-tail)

    @pl.loop(0, count // 32)
    def _(i):
        weigh(pl.ds(pl.multiple_of(i * 32, 32), 32), i * 32)

    def receive(w, i):
        @pl.when((i > 0) & (i < L))
        def _():
            l = me.order(i)
            arrived(w, l, side, core)
            spread(w, l, None, lambda c: c.start())

    def side_ready(w, l, mm):
        m = jnp.where(mm == 0, side, 1 - side)

        @pl.when(mm == 1)
        def _():
            arrived(w, l, m, core)
            copy(w, l, m, core, 3).start()

        arrived(w, l, m, 1 - core)
        return l * 2 + m

    zk[...] = jnp.zeros_like(zk)

    def keys_ready(which, buf, j):
        @pl.when((j < base) | (j >= base + FB))
        def _():
            remote(buf.at[j], buf.at[j], k_send.at[which, 0, 0], k_recv.at[which, j], peers[0]).wait_recv()

    @pl.loop(0, L + 1)
    def _(i):
        receive(0, i)

        @pl.when(i == L - 1)
        def _():
            start_own(1)

        @pl.when(i > 0)
        def _():
            l = me.order(i - 1)

            @pl.loop(0, 2)
            def _(mm):
                j = side_ready(0, l, mm)
                keys_ready(0, keys, j)
                zk[...] += dot(keys[j], W[0, j])

    keys_out = pltpu.make_async_copy(keys, xx_out.at[0], out_sem.at[0])
    keys_out.start()
    values_out = pltpu.make_async_copy(values, v_out, out_sem.at[1])
    values_out.start()
    query_out = pltpu.make_async_copy(query.at[pl.ds(base, FB)], q_out, out_sem.at[2])
    query_out.start()

    def hide(rows):
        hid = jax.nn.silu(zk[rows, :]).astype(BF16)
        hk[rows, :] = hid
        wh[rows, :] = (weight[rows, :] * hid.astype(F32)).astype(BF16)

    rows_loop(count, 16, hide)
    wh_out = pltpu.make_async_copy(wh, yy_out.at[1], out_sem.at[3])
    wh_out.start()

    def ecopy(j, p):
        return remote(errs.at[head, j], errs.at[head, j], e_send.at[p, j], e_recv.at[head, j], peers[p])

    @pl.loop(0, L + 2)
    def _(i):
        receive(1, i)

        @pl.when(i == 1)
        def _():
            @pl.loop(0, chips)
            def _(j):
                keys_ready(1, query, j)

            zz[...] = jnp.zeros_like(zz)

            @pl.loop(0, chips)
            def _(j):
                zz[...] += dot(query[j], W[0, j])

            def hide_query(rows):
                hq[rows, :] = jax.nn.silu(zz[rows, :]).astype(BF16)

            rows_loop(count, 16, hide_query)
            zz[...] = jnp.zeros_like(zz)

        @pl.when((i > 0) & (i <= L))
        def _():
            l = me.order(i - 1)

            @pl.loop(0, 2)
            def _(mm):
                j = side_ready(1, l, mm)
                part = dot_nt(hk[...], W[1, j])
                mine = (j >= base) & (j < base + FB)

                @pl.when(mine)
                def _():
                    errs[head, j] = (part - values[j - base].astype(F32)).astype(BF16)

                @pl.when(jnp.logical_not(mine))
                def _():
                    errs[head, j] = part.astype(BF16)

                for p in range(n_head - 1):
                    ecopy(j, p).start()
                recall[j] = dot_nt(hq[...], W[1, j]).astype(BF16)

        @pl.when(i > 1)
        def _():
            l = me.order(i - 2)

            @pl.loop(0, 2)
            def _(mm):
                j = l * 2 + jnp.where(mm == 0, side, 1 - side)
                for by in range(1, n_head):
                    other = (head + by) % n_head
                    remote(
                        errs.at[other, j], errs.at[other, j], e_send.at[0, j], e_recv.at[other, j], peers[0]
                    ).wait_recv()
                total = errs[0, j].astype(F32)
                for p in range(1, n_head):
                    total = total + errs[p, j].astype(F32)
                err[j] = total.astype(BF16)
                zz[...] += dot(err[j], W[1, j])

    err_out = pltpu.make_async_copy(err, xx_out.at[1], out_sem.at[4])
    err_out.start()
    recall_copy = pltpu.make_async_copy(recall, recall_out, out_sem.at[5])
    recall_copy.start()

    def pull(rows):
        z = zk[rows, :]
        s = jax.nn.sigmoid(z)
        dz = zz[rows, :] * s * (1.0 + z * (1.0 - s))
        hk[rows, :] = (weight[rows, :] * dz).astype(BF16)

    rows_loop(count, 16, pull)
    wdz_out = pltpu.make_async_copy(hk, yy_out.at[0], out_sem.at[6])
    wdz_out.start()

    for c in fcopies:
        c.wait_send()

    @pl.loop(0, FB)
    def _(b):
        for which, buf in enumerate((keys, query)):
            for p in range(n_head - 1):
                xcopy(which, buf, b, p).wait_send()

    @pl.loop(0, chips)
    def _(j):
        for p in range(n_head - 1):
            ecopy(j, p).wait_send()

    @pl.loop(0, L)
    def _(l):
        for w in range(2):
            spread(w, l, None, lambda c: c.wait_send())
            copy(w, l, 1 - side, core, 3).wait_send()

    for c in (keys_out, values_out, query_out, wh_out, err_out, recall_copy, wdz_out):
        c.wait()


def forward(tok, qkv, own, rate_w, forget, n_seq, n_head, lr_scale):
    count, width = tok.shape
    _, R, H = own.shape
    F = qkv.shape[2]
    chips, wide = n_seq // 2, 2 * R
    FB = F // wide
    assert n_seq % 4 == 0 and n_seq >= 8 and FB * wide == F and chips * wide == width
    anywhere = pl.BlockSpec(memory_space=pl.ANY)
    vmem = pl.BlockSpec(memory_space=pltpu.VMEM)
    S = jax.ShapeDtypeStruct
    dma = pltpu.SemaphoreType.DMA
    return pl.pallas_call(
        functools.partial(forward_kernel, n_seq, n_head, lr_scale),
        out_shape=(
            S((2, chips, count, wide), BF16),
            S((2, count, H), BF16),
            S((FB, count, wide), BF16),
            S((FB, count, wide), BF16),
            S((chips, count, wide), BF16),
        ),
        in_specs=[vmem, anywhere, vmem, vmem, vmem],
        out_specs=(anywhere,) * 5,
        scratch_shapes=[
            pltpu.VMEM((2, chips, wide, H), BF16),
            pltpu.VMEM((2, width, F), BF16),
            pltpu.VMEM((chips, count, wide), BF16),
            pltpu.VMEM((chips, count, wide), BF16),
            pltpu.VMEM((FB, count, wide), BF16),
            pltpu.VMEM((count, H), F32),
            pltpu.VMEM((count, H), F32),
            pltpu.VMEM((count, H), BF16),
            pltpu.VMEM((count, H), BF16),
            pltpu.VMEM((count, H), BF16),
            pltpu.VMEM((n_head, chips, count, wide), BF16),
            pltpu.VMEM((chips, count, wide), BF16),
            pltpu.VMEM((chips, count, wide), BF16),
            pltpu.VMEM((count, 1), F32),
            pltpu.VMEM((n_seq, 1, count), F32),
            dma((2, 4, chips)),
            dma((2, n_seq)),
            dma((n_seq,)),
            dma((n_seq,)),
            dma((2, max(n_head - 1, 1), FB)),
            dma((2, chips)),
            dma((max(n_head - 1, 1), chips)),
            dma((n_head, chips)),
            dma((3,)),
            dma((7,)),
        ],
        compiler_params=pltpu.CompilerParams(
            collective_id=0, has_side_effects=True, vmem_limit_bytes=VMEM_LIMIT
        ),
    )(tok, qkv, own, rate_w, forget)


def backward_kernel(
    n_seq, n_head,
    xx_in, yy_in, q_in, v_in, recall_in, persist,
    grad, attended,
    xx, yy, query, values, recall, got, recalled, G, from_core, from_side, from_left, from_right, acc,
    c_send, c_recv, s_send, s_recv, z_send, l_recv, r_recv, x_send, x_recv, in_sem,
):
    me = Place(n_seq, n_head)
    L, line, side, core, head = me.length, me.line, me.side, me.core, me.head
    count, wide = xx.shape[2], xx.shape[3]
    R, H = acc.shape
    FB = query.shape[0]
    base = head * FB
    peers = me.peers()

    pairs = (
        (recall_in, recall), (xx_in.at[1], xx.at[1]), (yy_in.at[1], yy.at[1]), (xx_in.at[0], xx.at[0]),
        (yy_in.at[0], yy.at[0]), (q_in, query), (v_in, values),
    )
    loads = [pltpu.make_async_copy(a, b, in_sem.at[i]) for i, (a, b) in enumerate(pairs)]
    for c in loads:
        c.start()

    barrier = pltpu.get_barrier_semaphore()

    def greet(where):
        pl.semaphore_signal(barrier, inc=1, device_id=where, device_id_type=MESH)

    greet(me.at(line, side, 1 - core))
    greet(me.at(line, 1 - side, core))

    @pl.when(line > 0)
    def _():
        greet(me.at(line - 1, side, core))

    @pl.when(line < L - 1)
    def _():
        greet(me.at(line + 1, side, core))

    for peer in peers:
        greet(peer)
    ends = jnp.where(line > 0, 1, 0) + jnp.where(line < L - 1, 1, 0)
    pl.semaphore_wait(barrier, 2 + n_head - 1 + ends)

    def rcopy(b, p):
        there = peers[p]["head"] * FB
        return remote(recall.at[there + b], got.at[head, b], x_send.at[p, b], x_recv.at[head, b], peers[p])

    loads[0].wait()

    @pl.loop(0, FB)
    def _(b):
        for p in range(n_head - 1):
            rcopy(b, p).start()

    for c in loads[1:5]:
        c.wait()

    mine = pl.ds(pl.multiple_of(core * R, R), R)
    theirs = pl.ds(pl.multiple_of((1 - core) * R, R), R)

    def core_copy(w, j):
        return remote(
            G.at[w, j, theirs, :], from_core.at[w, j], c_send.at[w, j], c_recv.at[w, j],
            me.at(line, side, 1 - core),
        )

    def side_copy(w, l):
        return remote(
            G.at[w, l * 2 + 1 - side, mine, :], from_side.at[w, l], s_send.at[w, l], s_recv.at[w, l],
            me.at(line, 1 - side, core),
        )

    def right_copy(w, l):
        return remote(
            G.at[w, l * 2 + side, mine, :], from_left.at[w, l], z_send.at[w, l], l_recv.at[w, l],
            me.at(line + 1, side, core),
        )

    def left_copy(w, l):
        return remote(
            G.at[w, l * 2 + side, mine, :], from_right.at[w, l], z_send.at[w, l], r_recv.at[w, l],
            me.at(line - 1, side, core),
        )

    def partial(w, j):
        G[w, j] = dot_tn(xx[w, j], yy[w]).astype(BF16)
        core_copy(w, j).start()

    @pl.loop(0, 2 * L + 1)
    def _(n):
        @pl.when(n < 2 * L)
        def _():
            partial(1 - n // L, me.order(L - 1 - n % L) * 2 + 1 - side)

        @pl.when(n > 0)
        def _():
            w, l = 1 - (n - 1) // L, me.order(L - 1 - (n - 1) % L)
            j = l * 2 + 1 - side
            core_copy(w, j).wait_recv()
            both = G[w, j, mine, :].astype(F32) + from_core[w, j].astype(F32)
            G[w, j, mine, :] = both.astype(BF16)
            side_copy(w, l).start()

    heads_here = FB * wide // HEAD_DIM
    per = wide // HEAD_DIM
    chunk = count // 2
    scale = HEAD_DIM ** (-0.5)
    persist_count = persist.shape[1]

    def attend(n):
        b = n // per
        cols = pl.ds(pl.multiple_of((n % per) * HEAD_DIM, HEAD_DIM), HEAD_DIM)
        flat = pl.ds(pl.multiple_of(n * HEAD_DIM, HEAD_DIM), HEAD_DIM)
        for part in range(2):
            seen = (part + 1) * chunk
            q = query[b, pl.ds(part * chunk, chunk), cols]
            row = lax.broadcasted_iota(jnp.int32, (chunk, seen), 0) + part * chunk
            visible = lax.broadcasted_iota(jnp.int32, (chunk, seen), 1) <= row
            rec = recalled[b, pl.ds(0, seen), cols]
            key = xx[0, base + b, pl.ds(0, seen), cols]
            val = values[b, pl.ds(0, seen), cols]
            s0 = dot_nt(q, persist[0, :, flat]) * scale
            s1 = jnp.where(visible, dot_nt(q, rec) * scale, -1e30)
            s2 = jnp.where(visible, dot_nt(q, key) * scale, -1e30)
            top = jnp.maximum(
                jnp.max(s0, axis=1, keepdims=True),
                jnp.maximum(jnp.max(s1, axis=1, keepdims=True), jnp.max(s2, axis=1, keepdims=True)),
            )
            e0, e1, e2 = jnp.exp(s0 - top), jnp.exp(s1 - top), jnp.exp(s2 - top)
            norm = 1.0 / (
                jnp.sum(e0, axis=1, keepdims=True)
                + jnp.sum(e1, axis=1, keepdims=True)
                + jnp.sum(e2, axis=1, keepdims=True)
            )
            out = dot((e0 * norm).astype(BF16), persist[1, :, flat])
            out = out + dot((e1 * norm).astype(BF16), rec)
            out = out + dot((e2 * norm).astype(BF16), val)
            attended[pl.ds(part * chunk, chunk), flat] = out.astype(BF16)

    each = -(-heads_here // (2 * L))

    @pl.loop(0, 2 * L)
    def _(n):
        w, l = 1 - n // L, me.order(L - 1 - n % L)
        j = l * 2 + side
        partial(w, j)
        core_copy(w, j).wait_recv()
        remote(
            from_side.at[w, l], from_side.at[w, l], s_send.at[w, l], s_recv.at[w, l], me.at(line, 1 - side, core)
        ).wait_recv()
        acc[...] = G[w, j, mine, :].astype(F32) + from_core[w, j].astype(F32) + from_side[w, l].astype(F32)

        @pl.when((l >= line) & (line > 0))
        def _():
            remote(
                from_left.at[w, l], from_left.at[w, l], z_send.at[w, l], l_recv.at[w, l],
                me.at(line - 1, side, core),
            ).wait_recv()
            acc[...] += from_left[w, l].astype(F32)

        @pl.when((l <= line) & (line < L - 1))
        def _():
            remote(
                from_right.at[w, l], from_right.at[w, l], z_send.at[w, l], r_recv.at[w, l],
                me.at(line + 1, side, core),
            ).wait_recv()
            acc[...] += from_right[w, l].astype(F32)

        @pl.when(l == line)
        def _():
            grad[w] = acc[...]

        @pl.when(l != line)
        def _():
            G[w, j, mine, :] = acc[...].astype(BF16)

        @pl.when(l > line)
        def _():
            right_copy(w, l).start()

        @pl.when(l < line)
        def _():
            left_copy(w, l).start()

        @pl.when(n == 0)
        def _():
            loads[5].wait()
            loads[6].wait()

            @pl.loop(0, FB)
            def _(b):
                total = recall[base + b].astype(F32)
                for by in range(1, n_head):
                    other = (head + by) % n_head
                    remote(
                        got.at[other, b], got.at[other, b], x_send.at[0, b], x_recv.at[other, b], peers[0]
                    ).wait_recv()
                    total = total + got[other, b].astype(F32)
                recalled[b] = total.astype(BF16)

        for k in range(each):
            @pl.when(n * each + k < heads_here)
            def _():
                attend(n * each + k)

    @pl.loop(0, FB)
    def _(b):
        for p in range(n_head - 1):
            rcopy(b, p).wait_send()

    @pl.loop(0, L)
    def _(l):
        for w in range(2):
            core_copy(w, l * 2).wait_send()
            core_copy(w, l * 2 + 1).wait_send()
            side_copy(w, l).wait_send()

            @pl.when(l > line)
            def _():
                right_copy(w, l).wait_send()

            @pl.when(l < line)
            def _():
                left_copy(w, l).wait_send()


def backward(xx, yy, query, values, recall, persist, n_seq, n_head, R):
    _, chips, count, wide = xx.shape
    H, FB = yy.shape[2], query.shape[0]
    L = n_seq // 4
    anywhere = pl.BlockSpec(memory_space=pl.ANY)
    vmem = pl.BlockSpec(memory_space=pltpu.VMEM)
    S = jax.ShapeDtypeStruct
    dma = pltpu.SemaphoreType.DMA
    return pl.pallas_call(
        functools.partial(backward_kernel, n_seq, n_head),
        out_shape=(S((2, R, H), F32), S((count, FB * wide), BF16)),
        in_specs=[anywhere] * 5 + [vmem],
        out_specs=(vmem, vmem),
        scratch_shapes=[
            pltpu.VMEM((2, chips, count, wide), BF16),
            pltpu.VMEM((2, count, H), BF16),
            pltpu.VMEM((FB, count, wide), BF16),
            pltpu.VMEM((FB, count, wide), BF16),
            pltpu.VMEM((chips, count, wide), BF16),
            pltpu.VMEM((n_head, FB, count, wide), BF16),
            pltpu.VMEM((FB, count, wide), BF16),
            pltpu.VMEM((2, chips, wide, H), BF16),
            pltpu.VMEM((2, chips, R, H), BF16),
            pltpu.VMEM((2, L, R, H), BF16),
            pltpu.VMEM((2, L, R, H), BF16),
            pltpu.VMEM((2, L, R, H), BF16),
            pltpu.VMEM((R, H), F32),
            dma((2, chips)),
            dma((2, chips)),
            dma((2, L)),
            dma((2, L)),
            dma((2, L)),
            dma((2, L)),
            dma((2, L)),
            dma((max(n_head - 1, 1), FB)),
            dma((n_head, FB)),
            dma((7,)),
        ],
        compiler_params=pltpu.CompilerParams(
            collective_id=1, has_side_effects=True, vmem_limit_bytes=VMEM_LIMIT
        ),
    )(xx, yy, query, values, recall, persist)


def on_device(
    tokens, qkv_weight, persistent, rate_weight, forget_rate, momentum_decay, forget_share, memory, momentum
):
    n_seq, n_head = lax.axis_size("seq"), lax.axis_size("head")
    seg_len, width = tokens.shape[1], tokens.shape[2]
    lr_scale = 2.0 / (width * n_seq * seg_len) ** 0.5
    own = jnp.transpose(memory.astype(BF16), (1, 0, 2))
    qkv = jnp.transpose(qkv_weight, (1, 0, 2))
    xx, yy, query, values, recall = forward(
        tokens[0], qkv, own, rate_weight[None], forget_rate, n_seq, n_head, lr_scale
    )
    grad, attended = backward(xx, yy, query, values, recall, persistent, n_seq, n_head, memory.shape[0])
    grad = jnp.transpose(grad, (1, 0, 2))
    momentum = momentum_decay[0] * momentum - grad
    memory = (1.0 - forget_share[0]) * memory + momentum
    return (attended[None], memory, momentum)


def solution(mesh):
    placed = (
        P(None, "seq", None),
        P(None, None, "head"),
        P(None, None, "head"),
        P(),
        P(None, "seq"),
        P(),
        P(),
        P("seq", None, "head"),
        P("seq", None, "head"),
    )
    return jax.shard_map(
        on_device,
        mesh=mesh,
        in_specs=placed,
        out_specs=(P(None, "seq", "head"), P("seq", None, "head"), P("seq", None, "head")),
        check_vma=False,
    )
```

profile of v0, /device:TPU:11, one launch (start us, length us, event | category | flops | bytes accessed | tf_op | source)
XLA Modules:
  0.0 269.5 jit_solution(8062744608560091627)
XLA Ops:
  0.6 3.7 %copy.25 = bf16[128,2,2048]{2,0,1:T(8,128)(2,1)} copy(f32[128,2,2048]{2,1,0:T(2,128)} %param.16) | data formatting | bytes 3145728 | tf_op args[7]
  4.3 124.5 %shard_map.112 = (bf16[2,8,512,256]{3,2,1,0:T(8,128)(2,1)}, bf16[2,512,2048]{2,1,0:T(8,128)(2,1)}, bf16[4,512,256]{2,1,0:T(8,128)(2,1)}, bf16[4,512,256]{2,1,0:T(8,128)(2,1)}, bf16[8,512,256]{2,1,0:T(8,128)(2,1)}) custom-call(bf16[512,2048]{1,0:T(8,128)(2,1)} %bitcast.15, bf16[3,2048,1024]{2,1,0:T(8,128)(2,1)} %bitcast.13, bf16[2,128,2048]{2,1,0:T(8,128)(2,1)} %bitcast.14, ...), custom_call_target="tpu_custom_call" | custom-call | tf_op jit(solution)/shard_map/pallas_call | solution.py:360
  128.8 127.1 %shard_map.113 = (f32[2,128,2048]{2,1,0:T(8,128)}, bf16[512,1024]{1,0:T(8,128)(2,1)}) custom-call(bf16[2,8,512,256]{3,2,1,0:T(8,128)(2,1)} %get-tuple-element.10.xx_in, bf16[2,512,2048]{2,1,0:T(8,128)(2,1)} %get-tuple-element.11.yy_in, bf16[4,512,256]{2,1,0:T(8,128)(2,1)} %get-tuple-element.12.q_in, bf16[4,512,256]{2,1,0:T(8,128)(2,1)} %get-tuple-element.13.v_in, ...), custom_call_target="tpu_custom_call" | custom-call | tf_op jit(solution)/shard_map/pallas_call | solution.py:639
  257.3 5.3 %multiply_add_fusion = (f32[128,2,2048]{2,0,1:T(8,128)S(1)}, f32[128,2,2048]{2,0,1:T(8,128)S(1)}) fusion(f32[128,2,2048]{2,1,0:T(2,128)} %param.16, f32[]{:T(128)} %bitcast.5, f32[2,128,2048]{2,1,0:T(8,128)} %get-tuple-element.16, f32[128,2,2048]{2,1,0:T(2,128)} %param.17, f32[]{:T(128)} %bitcast.12), kind=kLoop, calls=%fused_computation.2 | loop fusion | flops 2097152 | bytes 10485768 | tf_op jit(solution)/shard_map/add | solution.py:689
  262.6 2.9 %copy.15 = f32[128,2,2048]{2,1,0:T(2,128)} copy(f32[128,2,2048]{2,0,1:T(8,128)S(1)} %get-tuple-element.20) | data formatting | bytes 4194304
  265.5 0.0 copy-start
  265.5 2.9 %copy.16 = f32[128,2,2048]{2,1,0:T(2,128)} copy(f32[128,2,2048]{2,0,1:T(8,128)S(1)} %get-tuple-element.21) | data formatting | bytes 4194304
  268.5 0.0 copy-done
  268.5 1.0 copy.29
Async XLA Ops:
  265.5 2.9 %copy-start = (bf16[512,1024]{1,0:T(8,128)(2,1)S(1)}, bf16[512,1024]{1,0:T(8,128)(2,1)}, u32[]{:S(2)}) copy-start(bf16[512,1024]{1,0:T(8,128)(2,1)} %get-tuple-element.15) | copy-start | bytes 3145732
where the time goes:
time: 273 us; the launch traced here: 269 us
  Pallas kernels  252 us (92%)
  local copies, waits for them, and re-layouts  10.5 us (4%)
  other arithmetic  5.35 us (2%)
    pallas_call x1, Pallas kernels, backward(): pl.pallas_call(functools.partial(backward_kernel, n_seq, n_head), out_sha...  127 us
    pallas_call x1, Pallas kernels, forward(): pl.pallas_call(functools.partial(forward_kernel, n_seq, n_head, lr_scale)...  125 us
    unnamed x6, local copies, waits for them, and re-layouts  10.5 us

commit v1 on v0

v1 whole, which is shorter than its diff:
```python
import functools

import jax
import jax.numpy as jnp
from jax import lax
from jax.experimental import pallas as pl
from jax.experimental.pallas import tpu as pltpu
from jax.sharding import PartitionSpec as P

HEAD_DIM = 128
LANES = 128
MESH = pl.DeviceIdType.MESH
VMEM_LIMIT = 67043328
PIECES = 2
EARLY = 2
F32, BF16 = jnp.float32, jnp.bfloat16


def remote(src, dst, send_sem, recv_sem, where):
    return pltpu.make_async_remote_copy(
        src_ref=src,
        dst_ref=dst,
        send_sem=send_sem,
        recv_sem=recv_sem,
        device_id=where,
        device_id_type=MESH,
    )


def dot(a, b):
    return jnp.dot(a, b, preferred_element_type=F32)


def dot_nt(a, b):
    return lax.dot_general(a, b, (((1,), (1,)), ((), ())), preferred_element_type=F32)


def dot_tn(a, b):
    return lax.dot_general(a, b, (((0,), (0,)), ((), ())), preferred_element_type=F32)


class Place:
    def __init__(self, n_seq, n_head):
        self.n_seq, self.n_head = n_seq, n_head
        self.length = n_seq // 4
        self.seq, self.head = lax.axis_index("seq"), lax.axis_index("head")
        self.line = self.seq // 4
        self.side = (self.seq // 2) % 2
        self.core = self.seq % 2

    def at(self, line, side, core):
        return {"seq": (line * 2 + side) * 2 + core}

    def order(self, i):
        left, right = self.line, self.length - 1 - self.line
        both = jnp.minimum(left, right)
        paired = i <= 2 * both
        step = jnp.where(paired, (i + 1) // 2, i - both)
        to_left = jnp.where(paired, i % 2 == 1, left > right)
        return jnp.where(to_left, self.line - step, self.line + step)

    def peers(self):
        return [{"head": (self.head + by) % self.n_head} for by in range(1, self.n_head)]


def rows_loop(total, step, body):
    @pl.loop(0, total // step)
    def _(i):
        body(pl.ds(pl.multiple_of(i * step, step), step))


def forward_kernel(
    n_seq, n_head, lr_scale,
    tok, qkv, memory, rate_w, forget,
    xx_out, yy_out, q_out, v_out, recall_out, g_out,
    staged, own, W, wbuf, keys, query, values, zk, zz, hk, hq, wh, errs, recall, weight, frb, G, from_core, from_side,
    w_send, w_recv, f_send, f_recv, k_send, k_recv, e_send, e_recv, qkv_sem, out_sem, block_sem, g_send, g_recv, mem_sem,
):
    me = Place(n_seq, n_head)
    L, line, side, core, head = me.length, me.line, me.side, me.core, me.head
    chips = n_seq // 2
    count, width = tok.shape
    R, H = own.shape[1:]
    wide = 2 * R
    FB = values.shape[0]
    base = head * FB
    peers = me.peers()

    memory_load = pltpu.make_async_copy(memory, staged, mem_sem)
    memory_load.start()
    loads = [pltpu.make_async_copy(qkv.at[k], wbuf.at[s], qkv_sem.at[k]) for k, s in ((1, 0), (0, 1), (2, 0))]
    loads[0].start()
    loads[1].start()

    barrier = pltpu.get_barrier_semaphore()
    for by in range(1, n_seq):
        pl.semaphore_signal(barrier, inc=1, device_id={"seq": (me.seq + by) % n_seq}, device_id_type=MESH)
    for peer in peers:
        pl.semaphore_signal(barrier, inc=1, device_id=peer, device_id_type=MESH)
    memory_load.wait()
    each = 2 * H // LANES
    for k in range(2):
        for tile in range(H // LANES):
            tiles = staged[pl.ds(tile * 2 + k, R, stride=each), :]
            own[k, :, tile * LANES : (tile + 1) * LANES] = tiles.astype(BF16)
    pl.semaphore_wait(barrier, n_seq - 1 + n_head - 1)

    piece = R // PIECES

    def block(w, l, m, c, p):
        return W.at[w, l * 2 + m, pl.ds(pl.multiple_of(c * R + p * piece, piece), piece), :]

    def copy(w, l, m, c, p, way, mine=False):
        where = (
            me.at(line + 1, side, core),
            me.at(line - 1, side, core),
            me.at(line, 1 - side, core),
            me.at(line, side, 1 - core),
        )[way]
        dst = block(w, l, m, c, p)
        src = own.at[w, pl.ds(pl.multiple_of(p * piece, piece), piece), :] if mine else dst
        chip = l * 2 + m
        return remote(src, dst, w_send.at[w, way, chip, p], w_recv.at[w, chip * 2 + c, p], where)

    def spread(w, l, p, act, ways=(0, 1, 2, 3), mine=False):
        if 0 in ways:

            @pl.when((l <= line) & (line < L - 1))
            def _():
                act(copy(w, l, side, core, p, 0, mine))

        if 1 in ways:

            @pl.when((l >= line) & (line > 0))
            def _():
                act(copy(w, l, side, core, p, 1, mine))

        for way in (2, 3):
            if way in ways:
                act(copy(w, l, side, core, p, way, mine))

    def start(c):
        c.start()

    def arrived(w, l, m, c, p):
        copy(w, l, m, c, p, 2).wait_recv()

    def start_own(w, ways):
        for p in range(PIECES):
            spread(w, line, p, start, ways, True)

    for p in range(PIECES):
        spread(0, line, p, start, (0, 1, 3), True)
    spread(0, line, 0, start, (2,), True)
    fcopies = []
    for by in range(1, n_seq):
        fcopies.append(
            remote(forget, frb.at[me.seq], f_send.at[by], f_recv.at[me.seq], {"seq": (me.seq + by) % n_seq})
        )
    for c in fcopies:
        c.start()
    frb[me.seq] = forget[...]

    def xcopy(which, buf, b, p):
        return remote(
            buf.at[base + b], buf.at[base + b], k_send.at[which, p, b], k_recv.at[which, base + b], peers[p]
        )

    def project(slot, b):
        cols = pl.ds(pl.multiple_of(b * wide, wide), wide)
        return dot(tok[...], wbuf[slot, :, cols]).astype(BF16)

    def project_shared(which, buf, slot):
        loads[which].wait()

        @pl.loop(0, FB)
        def _(b):
            buf[base + b] = project(slot, b)
            for p in range(n_head - 1):
                xcopy(which, buf, b, p).start()

    def project_values():
        loads[2].wait()

        @pl.loop(0, FB)
        def _(b):
            values[b] = project(0, b)

    def weigh(rows, start_row, later):
        x = tok[rows, :].astype(F32)
        rate = jnp.sum(x * rate_w[...], axis=1, keepdims=True)
        n = x.shape[0]
        t = lax.broadcasted_iota(jnp.int32, (n, count), 0) + start_row
        u = lax.broadcasted_iota(jnp.int32, (n, count), 1)
        tail = jnp.sum(jnp.where(u > t, forget[...], 0.0), axis=1, keepdims=True) + later
        weight[rows, :] = lr_scale * jax.nn.sigmoid(rate) * jnp.exp(-tail)

    def weigh_all():
        for by in range(1, n_seq):
            other = (me.seq + by) % n_seq
            remote(forget, frb.at[other], f_send.at[by], f_recv.at[other], {"seq": other}).wait_recv()
        totals = jnp.sum(frb[...], axis=2, keepdims=True)
        which_seq = lax.broadcasted_iota(jnp.int32, totals.shape, 0)
        later = jnp.sum(jnp.where(which_seq > me.seq, totals, 0.0), axis=(0, 1, 2), keepdims=True)[0]

        @pl.loop(0, count // 32)
        def _(i):
            weigh(pl.ds(pl.multiple_of(i * 32, 32), 32), i * 32, later)

    for w in range(2):
        W[w, line * 2 + side, pl.ds(pl.multiple_of(core * R, R), R), :] = own[w]
    zk[...] = jnp.zeros_like(zk)
    right = L - 1 - line

    def keys_ready(which, buf, j):
        @pl.when((j < base) | (j >= base + FB))
        def _():
            remote(buf.at[j], buf.at[j], k_send.at[which, 0, 0], k_recv.at[which, j], peers[0]).wait_recv()

    def chip(l, mm):
        return l * 2 + jnp.where(mm == 0, side, 1 - side)

    def other_core(w, l, mm):
        for p in range(PIECES):
            arrived(w, l, jnp.where(mm == 0, side, 1 - side), 1 - core, p)

    def ecopy(j, p):
        return remote(errs.at[head, j], errs.at[head, j], e_send.at[p, j], e_recv.at[head, j], peers[p])

    def move(k):
        def come(away, step, ways):
            each = away * PIECES

            @pl.when((k > 0) & (k <= 2 * each))
            def _():
                at = k - 1
                w = jnp.where(at >= each, 1, 0)
                at = at - w * each
                l = line + step * (1 + at // PIECES)
                arrived(w, l, side, core, at % PIECES)
                spread(w, l, at % PIECES, start, ways)

            @pl.when(k == each)
            def _():
                start_own(1, ways[:1])

        come(line, -1, (0, 3))
        come(right, 1, (1, 3))

        @pl.when(k == 1)
        def _():
            start_own(1, (3,))

        total = 2 * L * PIECES

        def entry(n):
            return n // (L * PIECES), me.order(n // PIECES % L), n % PIECES

        half = L * PIECES
        first = k + jnp.where(k < half, 1, 2)
        end = jnp.minimum(k + jnp.where(k < half - 1, 2, 3), total)

        @pl.loop(first, end)
        def _(n):
            w, l, p = entry(n)

            @pl.when(l == line)
            def _():
                spread(w, l, p, start, (2,), True)

            @pl.when(l != line)
            def _():
                spread(w, l, p, start, (2,))

        @pl.when((k > 0) & (k <= total))
        def _():
            w, l, p = entry(k - 1)
            arrived(w, l, 1 - side, core, p)
            copy(w, l, 1 - side, core, p, 3).start()

    def hide(rows):
        z = zk[rows, :]
        s = jax.nn.sigmoid(z)
        hid = (z * s).astype(BF16)
        hk[rows, :] = hid
        wh[rows, :] = (weight[rows, :] * hid.astype(F32)).astype(BF16)
        zk[rows, :] = weight[rows, :] * (s * (1.0 + z * (1.0 - s)))

    def hide_query(rows):
        hq[rows, :] = jax.nn.silu(zz[rows, :]).astype(BF16)

    keys_out = pltpu.make_async_copy(keys, xx_out.at[0], out_sem.at[0])
    values_out = pltpu.make_async_copy(values, v_out, out_sem.at[1])
    query_out = pltpu.make_async_copy(query.at[pl.ds(base, FB)], q_out, out_sem.at[2])
    wh_out = pltpu.make_async_copy(wh, yy_out.at[1], out_sem.at[3])

    def err_copy(j):
        return pltpu.make_async_copy(errs.at[head, j], xx_out.at[1, j], block_sem.at[0, j])

    def recall_copy(j):
        return pltpu.make_async_copy(recall.at[j], recall_out.at[j], block_sem.at[1, j])

    def add_first(i):
        @pl.loop(0, 2)
        def _(mm):
            l = me.order(i)
            other_core(0, l, mm)
            j = chip(l, mm)
            keys_ready(0, keys, j)
            zk[...] += dot(keys[j], W[0, j])

    def make_error(i, mm):
        @pl.when((i >= 0) & (i < L))
        def _():
            l = me.order(i)
            other_core(1, l, mm)
            j = chip(l, mm)
            part = dot_nt(hk[...], W[1, j])
            mine = (j >= base) & (j < base + FB)

            @pl.when(mine)
            def _():
                errs[head, j] = (part - values[j - base].astype(F32)).astype(BF16)

            @pl.when(jnp.logical_not(mine))
            def _():
                errs[head, j] = part.astype(BF16)

            for p in range(n_head - 1):
                ecopy(j, p).start()

    def make_recall(i):
        @pl.loop(0, 2)
        def _(mm):
            j = chip(me.order(i), mm)
            recall[j] = dot_nt(hq[...], W[1, j]).astype(BF16)
            recall_copy(j).start()

    def pull_error(i, mm):
        @pl.when((i >= 0) & (i < L))
        def _():
            j = chip(me.order(i), mm)
            for by in range(1, n_head):
                other = (head + by) % n_head
                remote(
                    errs.at[other, j], errs.at[other, j], e_send.at[0, j], e_recv.at[other, j], peers[0]
                ).wait_recv()
            total = errs[0, j].astype(F32)
            for p in range(1, n_head):
                total = total + errs[p, j].astype(F32)
            for p in range(n_head - 1):
                ecopy(j, p).wait_send()
            errs[head, j] = total.astype(BF16)
            err_copy(j).start()
            zz[...] += dot(errs[head, j], W[1, j])

    mine = pl.ds(pl.multiple_of(core * R, R), R)
    theirs = pl.ds(pl.multiple_of((1 - core) * R, R), R)

    def early_core(i):
        return remote(
            G.at[i, theirs, :], from_core.at[i], g_send.at[0, i], g_recv.at[0, i], me.at(line, side, 1 - core)
        )

    def early_side(i):
        return remote(
            G.at[i, mine, :], from_side.at[i], g_send.at[1, i], g_recv.at[1, i], me.at(line, 1 - side, core)
        )

    def early_partial(i):
        G[i] = dot_tn(errs[head, chip(me.order(i), 1)], wh[...]).astype(BF16)
        early_core(i).start()

    def early_on(i):
        early_core(i).wait_recv()
        G[i, mine, :] = (G[i, mine, :].astype(F32) + from_core[i].astype(F32)).astype(BF16)
        early_side(i).start()

    def add_query(low, high):
        @pl.loop(low, high)
        def _(j):
            keys_ready(1, query, j)
            zz[...] += dot(query[j], W[0, j])

    @pl.loop(0, PIECES * (2 * L + 1) + 1)
    def _(k):
        move(k)
        slot = k // PIECES
        even = k % PIECES == 0
        last = k % PIECES == PIECES - 1

        @pl.when(k == 0)
        def _():
            project_shared(0, keys, 0)
            loads[2].start()

        @pl.when(k == 1)
        def _():
            project_shared(1, query, 1)

        @pl.when(k == PIECES)
        def _():
            project_values()

        @pl.when(k == PIECES + 1)
        def _():
            weigh_all()

        @pl.when(even & (slot > 0) & (slot <= L))
        def _():
            add_first(slot - 1)

        @pl.when(k == PIECES * L)
        def _():
            keys_out.start()
            rows_loop(count, 16, hide)
            wh_out.start()
            zz[...] = jnp.zeros_like(zz)

        @pl.when(even & (slot >= L) & (slot <= 2 * L))
        def _():
            @pl.loop(jnp.where(slot == L, -1, 0), 2)
            def _(nth):
                mm = jnp.maximum(nth, 0)
                make_error(slot - L + jnp.where(nth < 0, 0, 1 - 2 * mm), mm)

        @pl.when(k == PIECES * L + 1)
        def _():
            add_query(0, chips // 2)

        @pl.when(k == PIECES * (L + 1) + 1)
        def _():
            add_query(chips // 2, chips)
            rows_loop(count, 16, hide_query)
            zz[...] = jnp.zeros_like(zz)
            values_out.start()
            query_out.start()

        @pl.when(last & (slot > L) & (slot <= 2 * L))
        def _():
            make_recall(slot - L - 1)

        @pl.when((last & (slot > L)) | (k == PIECES * (2 * L + 1)))
        def _():
            @pl.loop(jnp.where(slot == L + 1, -1, 0), 2)
            def _(nth):
                mm = jnp.maximum(nth, 0)
                pull_error(slot - L - jnp.where(nth < 0, 1, 2 * mm), mm)

        @pl.when(even & (slot > 2 * L - 2) & (slot <= 2 * L - 2 + EARLY))
        def _():
            early_on(slot - 2 * L + 1)

        @pl.when(last & (slot > 2 * L - 3) & (slot <= 2 * L - 3 + EARLY))
        def _():
            early_partial(slot - 2 * L + 2)


    def pull(rows):
        hk[rows, :] = (zz[rows, :] * zk[rows, :]).astype(BF16)

    rows_loop(count, 16, pull)
    wdz_out = pltpu.make_async_copy(hk, yy_out.at[0], out_sem.at[4])
    wdz_out.start()
    early_out = []
    for i in range(EARLY):
        early_side(i).wait_recv()
        early_out.append(pltpu.make_async_copy(from_side.at[i], g_out.at[i], out_sem.at[5 + i]))
        early_out[i].start()

    for c in fcopies:
        c.wait_send()

    @pl.loop(0, FB)
    def _(b):
        for which, buf in enumerate((keys, query)):
            for p in range(n_head - 1):
                xcopy(which, buf, b, p).wait_send()

    @pl.loop(0, L)
    def _(l):
        for w in range(2):
            for p in range(PIECES):
                spread(w, l, p, lambda c: c.wait_send())
                copy(w, l, 1 - side, core, p, 3).wait_send()

    for i in range(EARLY):
        early_core(i).wait_send()
        early_side(i).wait_send()

    @pl.loop(0, chips)
    def _(j):
        err_copy(j).wait()
        recall_copy(j).wait()

    for c in (keys_out, values_out, query_out, wh_out, wdz_out, *early_out):
        c.wait()


def forward(tok, qkv, memory, rate_w, forget, R, H, n_seq, n_head, lr_scale):
    count, width = tok.shape
    F = qkv.shape[2]
    chips, wide = n_seq // 2, 2 * R
    FB = F // wide
    assert n_seq % 4 == 0 and n_seq >= 16 and FB * wide == F and chips * wide == width
    anywhere = pl.BlockSpec(memory_space=pl.ANY)
    vmem = pl.BlockSpec(memory_space=pltpu.VMEM)
    S = jax.ShapeDtypeStruct
    dma = pltpu.SemaphoreType.DMA
    return pl.pallas_call(
        functools.partial(forward_kernel, n_seq, n_head, lr_scale),
        out_shape=(
            S((2, chips, count, wide), BF16),
            S((2, count, H), BF16),
            S((FB, count, wide), BF16),
            S((FB, count, wide), BF16),
            S((chips, count, wide), BF16),
            S((EARLY, R, H), BF16),
        ),
        in_specs=[vmem, anywhere, anywhere, vmem, vmem],
        out_specs=(anywhere,) * 6,
        scratch_shapes=[
            pltpu.VMEM(memory.shape, F32),
            pltpu.VMEM((2, R, H), BF16),
            pltpu.VMEM((2, chips, wide, H), BF16),
            pltpu.VMEM((2, width, F), BF16),
            pltpu.VMEM((chips, count, wide), BF16),
            pltpu.VMEM((chips, count, wide), BF16),
            pltpu.VMEM((FB, count, wide), BF16),
            pltpu.VMEM((count, H), F32),
            pltpu.VMEM((count, H), F32),
            pltpu.VMEM((count, H), BF16),
            pltpu.VMEM((count, H), BF16),
            pltpu.VMEM((count, H), BF16),
            pltpu.VMEM((n_head, chips, count, wide), BF16),
            pltpu.VMEM((chips, count, wide), BF16),
            pltpu.VMEM((count, 1), F32),
            pltpu.VMEM((n_seq, 1, count), F32),
            pltpu.VMEM((EARLY, wide, H), BF16),
            pltpu.VMEM((EARLY, R, H), BF16),
            pltpu.VMEM((EARLY, R, H), BF16),
            dma((2, 4, chips, PIECES)),
            dma((2, n_seq, PIECES)),
            dma((n_seq,)),
            dma((n_seq,)),
            dma((2, max(n_head - 1, 1), FB)),
            dma((2, chips)),
            dma((max(n_head - 1, 1), chips)),
            dma((n_head, chips)),
            dma((3,)),
            dma((5 + EARLY,)),
            dma((2, chips)),
            dma((2, EARLY)),
            dma((2, EARLY)),
            dma,
        ],
        compiler_params=pltpu.CompilerParams(
            collective_id=0, has_side_effects=True, vmem_limit_bytes=VMEM_LIMIT
        ),
    )(tok, qkv, memory, rate_w, forget)


def backward_kernel(
    n_seq, n_head,
    xx_in, yy_in, q_in, v_in, recall_in, g_in, persist,
    grad, attended,
    xx, yy, query, values, recall, got, recalled, G, from_core, from_side, from_left, from_right, acc,
    c_send, c_recv, s_send, s_recv, z_send, l_recv, r_recv, x_send, x_recv, in_sem,
):
    me = Place(n_seq, n_head)
    L, line, side, core, head = me.length, me.line, me.side, me.core, me.head
    count, wide = xx.shape[2], xx.shape[3]
    R, H = acc.shape
    FB = query.shape[0]
    base = head * FB
    peers = me.peers()

    pairs = (
        (recall_in, recall), (xx_in.at[1], xx.at[1]), (yy_in.at[1], yy.at[1]), (xx_in.at[0], xx.at[0]),
        (yy_in.at[0], yy.at[0]), (q_in, query), (v_in, values),
        *[(g_in.at[i], from_side.at[1, me.order(i)]) for i in range(EARLY)],
    )
    loads = [pltpu.make_async_copy(a, b, in_sem.at[i]) for i, (a, b) in enumerate(pairs)]
    for c in loads:
        c.start()

    barrier = pltpu.get_barrier_semaphore()

    def greet(where):
        pl.semaphore_signal(barrier, inc=1, device_id=where, device_id_type=MESH)

    greet(me.at(line, side, 1 - core))
    greet(me.at(line, 1 - side, core))

    @pl.when(line > 0)
    def _():
        greet(me.at(line - 1, side, core))

    @pl.when(line < L - 1)
    def _():
        greet(me.at(line + 1, side, core))

    for peer in peers:
        greet(peer)
    ends = jnp.where(line > 0, 1, 0) + jnp.where(line < L - 1, 1, 0)
    pl.semaphore_wait(barrier, 2 + n_head - 1 + ends)

    def rcopy(b, p):
        there = peers[p]["head"] * FB
        return remote(recall.at[there + b], got.at[head, b], x_send.at[p, b], x_recv.at[head, b], peers[p])

    loads[0].wait()

    @pl.loop(0, FB)
    def _(b):
        for p in range(n_head - 1):
            rcopy(b, p).start()

    for c in loads[1:3]:
        c.wait()

    mine = pl.ds(pl.multiple_of(core * R, R), R)
    theirs = pl.ds(pl.multiple_of((1 - core) * R, R), R)

    def core_copy(w, j):
        return remote(
            G.at[w, j, theirs, :], from_core.at[w, j], c_send.at[w, j], c_recv.at[w, j],
            me.at(line, side, 1 - core),
        )

    def side_copy(w, l):
        return remote(
            G.at[w, l * 2 + 1 - side, mine, :], from_side.at[w, l], s_send.at[w, l], s_recv.at[w, l],
            me.at(line, 1 - side, core),
        )

    def right_copy(w, l):
        return remote(
            G.at[w, l * 2 + side, mine, :], from_left.at[w, l], z_send.at[w, l], l_recv.at[w, l],
            me.at(line + 1, side, core),
        )

    def left_copy(w, l):
        return remote(
            G.at[w, l * 2 + side, mine, :], from_right.at[w, l], z_send.at[w, l], r_recv.at[w, l],
            me.at(line - 1, side, core),
        )

    def partial(w, j):
        G[w, j] = dot_tn(xx[w, j], yy[w]).astype(BF16)
        core_copy(w, j).start()

    there = 2 * L - EARLY

    def across(n):
        w = jnp.where(n < L - EARLY, 1, 0)
        return w, me.order(L - 1 - n + (1 - w) * (L - EARLY))

    @pl.loop(0, there + 1)
    def _(n):
        @pl.when(n == L - EARLY)
        def _():
            loads[3].wait()
            loads[4].wait()

        @pl.when(n < there)
        def _():
            w, l = across(n)
            partial(w, l * 2 + 1 - side)

        @pl.when(n > 0)
        def _():
            w, l = across(n - 1)
            j = l * 2 + 1 - side
            core_copy(w, j).wait_recv()
            both = G[w, j, mine, :].astype(F32) + from_core[w, j].astype(F32)
            G[w, j, mine, :] = both.astype(BF16)
            side_copy(w, l).start()

    for c in loads[5:]:
        c.wait()

    far = L - 1

    def along(n):
        w, at = 1 - n // far, n % far
        at_end = (w == 1) & ((line == 0) | (line == L - 1))
        i = jnp.where(at_end, jnp.where(at == 0, 1, L - at), L - 1 - at)
        own = n >= 2 * far
        return jnp.where(own, 1 - (n - 2 * far), w), jnp.where(own, 0, i)

    heads_here = FB * wide // HEAD_DIM
    per = wide // HEAD_DIM
    chunk = count // 2
    scale = HEAD_DIM ** (-0.5)
    persist_count = persist.shape[1]

    def attend(n):
        b = n // per
        cols = pl.ds(pl.multiple_of((n % per) * HEAD_DIM, HEAD_DIM), HEAD_DIM)
        flat = pl.ds(pl.multiple_of(n * HEAD_DIM, HEAD_DIM), HEAD_DIM)
        for part in range(2):
            seen = (part + 1) * chunk
            q = query[b, pl.ds(part * chunk, chunk), cols]
            row = lax.broadcasted_iota(jnp.int32, (chunk, seen), 0) + part * chunk
            visible = lax.broadcasted_iota(jnp.int32, (chunk, seen), 1) <= row
            rec = recalled[b, pl.ds(0, seen), cols]
            key = xx[0, base + b, pl.ds(0, seen), cols]
            val = values[b, pl.ds(0, seen), cols]
            s0 = dot_nt(q, persist[0, :, flat]) * scale
            s1 = jnp.where(visible, dot_nt(q, rec) * scale, -1e30)
            s2 = jnp.where(visible, dot_nt(q, key) * scale, -1e30)
            top = jnp.maximum(
                jnp.max(s0, axis=1, keepdims=True),
                jnp.maximum(jnp.max(s1, axis=1, keepdims=True), jnp.max(s2, axis=1, keepdims=True)),
            )
            e0, e1, e2 = jnp.exp(s0 - top), jnp.exp(s1 - top), jnp.exp(s2 - top)
            norm = 1.0 / (
                jnp.sum(e0, axis=1, keepdims=True)
                + jnp.sum(e1, axis=1, keepdims=True)
                + jnp.sum(e2, axis=1, keepdims=True)
            )
            out = dot((e0 * norm).astype(BF16), persist[1, :, flat])
            out = out + dot((e1 * norm).astype(BF16), rec)
            out = out + dot((e2 * norm).astype(BF16), val)
            attended[pl.ds(part * chunk, chunk), flat] = out.astype(BF16)

    def recall_all():
        @pl.loop(0, FB)
        def _(b):
            total = recall[base + b].astype(F32)
            for by in range(1, n_head):
                other = (head + by) % n_head
                remote(
                    got.at[other, b], got.at[other, b], x_send.at[0, b], x_recv.at[other, b], peers[0]
                ).wait_recv()
                total = total + got[other, b].astype(F32)
            recalled[b] = total.astype(BF16)

    each = -(-heads_here // 2)

    @pl.loop(0, 2 * L)
    def _(n):
        w, i = along(n)
        l = me.order(i)
        j = l * 2 + side
        partial(w, j)

        @pl.when(n == far)
        def _():
            recall_all()

        @pl.loop(jnp.maximum((n - far) * each, 0), jnp.clip((n - far + 1) * each, 0, heads_here))
        def _(k):
            attend(k)

        core_copy(w, j).wait_recv()

        @pl.when((w == 0) | (i >= EARLY))
        def _():
            remote(
                from_side.at[w, l], from_side.at[w, l], s_send.at[w, l], s_recv.at[w, l],
                me.at(line, 1 - side, core),
            ).wait_recv()

        acc[...] = G[w, j, mine, :].astype(F32) + from_core[w, j].astype(F32) + from_side[w, l].astype(F32)

        @pl.when((l >= line) & (line > 0))
        def _():
            remote(
                from_left.at[w, l], from_left.at[w, l], z_send.at[w, l], l_recv.at[w, l],
                me.at(line - 1, side, core),
            ).wait_recv()
            acc[...] += from_left[w, l].astype(F32)

        @pl.when((l <= line) & (line < L - 1))
        def _():
            remote(
                from_right.at[w, l], from_right.at[w, l], z_send.at[w, l], r_recv.at[w, l],
                me.at(line + 1, side, core),
            ).wait_recv()
            acc[...] += from_right[w, l].astype(F32)

        @pl.when(l == line)
        def _():
            grad[w] = acc[...]

        @pl.when(l != line)
        def _():
            G[w, j, mine, :] = acc[...].astype(BF16)

        @pl.when(l > line)
        def _():
            right_copy(w, l).start()

        @pl.when(l < line)
        def _():
            left_copy(w, l).start()

    @pl.loop(0, FB)
    def _(b):
        for p in range(n_head - 1):
            rcopy(b, p).wait_send()

    @pl.loop(0, there)
    def _(n):
        w, l = across(n)
        core_copy(w, l * 2 + 1 - side).wait_send()
        side_copy(w, l).wait_send()

    @pl.loop(0, L)
    def _(l):
        for w in range(2):
            core_copy(w, l * 2 + side).wait_send()

            @pl.when(l > line)
            def _():
                right_copy(w, l).wait_send()

            @pl.when(l < line)
            def _():
                left_copy(w, l).wait_send()


def backward(xx, yy, query, values, recall, early, persist, n_seq, n_head, R):
    _, chips, count, wide = xx.shape
    H, FB = yy.shape[2], query.shape[0]
    L = n_seq // 4
    anywhere = pl.BlockSpec(memory_space=pl.ANY)
    vmem = pl.BlockSpec(memory_space=pltpu.VMEM)
    S = jax.ShapeDtypeStruct
    dma = pltpu.SemaphoreType.DMA
    return pl.pallas_call(
        functools.partial(backward_kernel, n_seq, n_head),
        out_shape=(S((2, R, H), F32), S((count, FB * wide), BF16)),
        in_specs=[anywhere] * 6 + [vmem],
        out_specs=(vmem, vmem),
        scratch_shapes=[
            pltpu.VMEM((2, chips, count, wide), BF16),
            pltpu.VMEM((2, count, H), BF16),
            pltpu.VMEM((FB, count, wide), BF16),
            pltpu.VMEM((FB, count, wide), BF16),
            pltpu.VMEM((chips, count, wide), BF16),
            pltpu.VMEM((n_head, FB, count, wide), BF16),
            pltpu.VMEM((FB, count, wide), BF16),
            pltpu.VMEM((2, chips, wide, H), BF16),
            pltpu.VMEM((2, chips, R, H), BF16),
            pltpu.VMEM((2, L, R, H), BF16),
            pltpu.VMEM((2, L, R, H), BF16),
            pltpu.VMEM((2, L, R, H), BF16),
            pltpu.VMEM((R, H), F32),
            dma((2, chips)),
            dma((2, chips)),
            dma((2, L)),
            dma((2, L)),
            dma((2, L)),
            dma((2, L)),
            dma((2, L)),
            dma((max(n_head - 1, 1), FB)),
            dma((n_head, FB)),
            dma((7 + EARLY,)),
        ],
        compiler_params=pltpu.CompilerParams(
            collective_id=1, has_side_effects=True, vmem_limit_bytes=VMEM_LIMIT
        ),
    )(xx, yy, query, values, recall, early, persist)


def interleave(x):
    R, two, H = x.shape
    return x.reshape(R, two, H // LANES, LANES).transpose(0, 2, 1, 3).reshape(R * two * H // LANES, LANES)


def layered(x, R, H):
    return x.reshape(R, H // LANES, 2, LANES).transpose(0, 2, 1, 3).reshape(R, 2, H)


def update_kernel(decay, share, grad, memory, momentum, memory_out, momentum_out):
    _, rows, H = grad.shape
    each = 2 * H // LANES
    for k in range(2):
        for tile in range(H // LANES):
            at = pl.ds(tile * 2 + k, rows, stride=each)
            new = decay[0] * momentum[at, :] - grad[k, :, tile * LANES : (tile + 1) * LANES]
            momentum_out[at, :] = new
            memory_out[at, :] = (1.0 - share[0]) * memory[at, :] + new


def update(decay, share, grad, memory, momentum):
    _, R, H = grad.shape
    step = R // 4
    each = 2 * H // LANES
    smem = pl.BlockSpec(memory_space=pltpu.SMEM)
    flat = pl.BlockSpec((step * each, LANES), lambda i: (i, 0))
    out = jax.ShapeDtypeStruct((R * each, LANES), F32)
    new_memory, new_momentum = pl.pallas_call(
        update_kernel,
        grid=(4,),
        out_shape=(out, out),
        in_specs=[smem, smem, pl.BlockSpec((2, step, H), lambda i: (0, i, 0)), flat, flat],
        out_specs=(flat, flat),
    )(decay, share, grad, interleave(memory), interleave(momentum))
    return layered(new_memory, R, H), layered(new_momentum, R, H)


def on_device(
    tokens, qkv_weight, persistent, rate_weight, forget_rate, momentum_decay, forget_share, memory, momentum
):
    n_seq, n_head = lax.axis_size("seq"), lax.axis_size("head")
    seg_len, width = tokens.shape[1], tokens.shape[2]
    lr_scale = 2.0 / (width * n_seq * seg_len) ** 0.5
    R, _, H = memory.shape
    memory_tiles = interleave(memory)
    qkv = jnp.transpose(qkv_weight, (1, 0, 2))
    xx, yy, query, values, recall, early = forward(
        tokens[0], qkv, memory_tiles, rate_weight[None], forget_rate, R, H, n_seq, n_head, lr_scale
    )
    grad, attended = backward(xx, yy, query, values, recall, early, persistent, n_seq, n_head, R)
    memory, momentum = update(momentum_decay, forget_share, grad, memory, momentum)
    return (attended[None], memory, momentum)


def solution(mesh):
    placed = (
        P(None, "seq", None),
        P(None, None, "head"),
        P(None, None, "head"),
        P(),
        P(None, "seq"),
        P(),
        P(),
        P("seq", None, "head"),
        P("seq", None, "head"),
    )
    return jax.shard_map(
        on_device,
        mesh=mesh,
        in_specs=placed,
        out_specs=(P(None, "seq", "head"), P("seq", None, "head"), P("seq", None, "head")),
        check_vma=False,
    )
```

time: 273 us -> 232 us (0.85)
  Pallas kernels: 252 us -> 228 us
  local copies, waits for them, and re-layouts: 10.5 us -> 0.97 us
  other arithmetic: 5.35 us -> 0 us
    pallas_call x1, Pallas kernels: 127 us -> 93.4 us  [backward(): pl.pallas_call(functools.partial(backward_kernel, n_seq, n_head), out_sha...]
    unnamed x6 -> x3, local copies, waits for them, and re-layouts: 10.5 us -> 0.97 us
    pallas_call x0 -> x1, Pallas kernels: none -> 8.16 us  [update(): pl.pallas_call(update_kernel, grid=(4,), out_shape=(out, out), in_specs=[...]
    add x1 -> x0, other arithmetic: 5.35 us -> none  [on_device(): memory = (1.0 - forget_share[0]) * memory + momentum]
where the time goes in v1:
time: 232 us; the launch traced here: 230 us
  Pallas kernels  228 us (98%)
    pallas_call x1, Pallas kernels, forward(): pl.pallas_call(functools.partial(forward_kernel, n_seq, n_head, lr_scale)...  126 us
    pallas_call x1, Pallas kernels, backward(): pl.pallas_call(functools.partial(backward_kernel, n_seq, n_head), out_sha...  93.4 us
    pallas_call x1, Pallas kernels, update(): pl.pallas_call(update_kernel, grid=(4,), out_shape=(out, out), in_specs=[...  8.16 us

profile of v1, /device:TPU:11, one launch (start us, length us, event | category | flops | bytes accessed | tf_op | source)
XLA Modules:
  0.0 230.5 jit_solution(15131969573914855538)
XLA Ops:
  0.6 126.0 %shard_map.112 = (bf16[2,8,512,256]{3,2,1,0:T(8,128)(2,1)}, bf16[2,512,2048]{2,1,0:T(8,128)(2,1)}, bf16[4,512,256]{2,1,0:T(8,128)(2,1)}, bf16[4,512,256]{2,1,0:T...) custom-call(bf16[512,2048]{1,0:T(8,128)(2,1)} %bitcast.28, bf16[3,2048,1024]{2,1,0:T(8,128)(2,1)} %bitcast.24, ...), custom_call_target="tpu_custom_call" | custom-call | tf_op jit(solution)/shard_map/pallas_call | solution.py:510
  126.7 93.4 %shard_map.113 = (f32[2,128,2048]{2,1,0:T(8,128)}, bf16[512,1024]{1,0:T(8,128)(2,1)}) custom-call(bf16[2,8,512,256]{3,2,1,0:T(8,128)(2,1)} %get-tuple-element.13.xx_in, bf16[2,512,2048]{2,1,0:T(8,128)(2,1)} %get-tuple-element.14.yy_in, bf16[4,512,256]{2,1,0:T(8,128)(2,1)} %get-tuple-element.15.q_in, bf16[4,512,256]{2,1,0:T(8,128)(2,1)} %get-tuple-element.16.v_in, ...), custom_call_target="tpu_custom_call" | custom-call | tf_op jit(solution)/shard_map/pallas_call | solution.py:833
  221.3 0.0 copy-start
  221.3 8.2 %shard_map.114 = (f32[4096,128]{1,0:T(8,128)}, f32[4096,128]{1,0:T(8,128)}) custom-call(f32[1]{0:T(128)S(6)} %copy.17.decay, f32[1]{0:T(128)S(6)} %copy.18.share, f32[2,128,2048]{2,1,0:T(8,128)} %get-tuple-element.20.grad, f32[4096,128]{1,0:T(8,128)} %bitcast.26, f32[4096,128]{1,0:T(8,128)} %bitcast.27), custom_call_target="tpu_custom_call" | custom-call | tf_op jit(solution)/shard_map/pallas_call | solution.py:896
  229.5 0.0 copy-done
  229.5 1.0 copy.19
Async XLA Ops:
  221.3 8.2 %copy-start = (bf16[512,1024]{1,0:T(8,128)(2,1)S(1)}, bf16[512,1024]{1,0:T(8,128)(2,1)}, u32[]{:S(2)}) copy-start(bf16[512,1024]{1,0:T(8,128)(2,1)} %get-tuple-element.19) | copy-start | bytes 3145732

commit v2 on v1

--- a/solution.py
+++ b/solution.py
@@ -13,6 +13,7 @@
 VMEM_LIMIT = 67043328
 PIECES = 2
 EARLY = 2
+UPDATE_STEPS = 2
 F32, BF16 = jnp.float32, jnp.bfloat16
 
 
@@ -97,12 +98,13 @@
         pl.semaphore_signal(barrier, inc=1, device_id={"seq": (me.seq + by) % n_seq}, device_id_type=MESH)
     for peer in peers:
         pl.semaphore_signal(barrier, inc=1, device_id=peer, device_id_type=MESH)
+    def cast(k):
+        for tile in range(H // LANES):
+            tiles = staged[pl.ds(tile * 2 + k, R, stride=2 * H // LANES), :]
+            own[k, :, tile * LANES : (tile + 1) * LANES] = tiles.astype(BF16)
+
     memory_load.wait()
-    each = 2 * H // LANES
-    for k in range(2):
-        for tile in range(H // LANES):
-            tiles = staged[pl.ds(tile * 2 + k, R, stride=each), :]
-            own[k, :, tile * LANES : (tile + 1) * LANES] = tiles.astype(BF16)
+    cast(0)
     pl.semaphore_wait(barrier, n_seq - 1 + n_head - 1)
 
     piece = R // PIECES
@@ -152,6 +154,7 @@
     for p in range(PIECES):
         spread(0, line, p, start, (0, 1, 3), True)
     spread(0, line, 0, start, (2,), True)
+    cast(1)
     fcopies = []
     for by in range(1, n_seq):
         fcopies.append(
@@ -581,7 +584,7 @@
         *[(g_in.at[i], from_side.at[1, me.order(i)]) for i in range(EARLY)],
     )
     loads = [pltpu.make_async_copy(a, b, in_sem.at[i]) for i, (a, b) in enumerate(pairs)]
-    for c in loads:
+    for c in (loads[1], loads[2], loads[0], *loads[3:]):
         c.start()
 
     barrier = pltpu.get_barrier_semaphore()
@@ -651,14 +654,86 @@
         core_copy(w, j).start()
 
     there = 2 * L - EARLY
+    far = L - 1
+    at_end = (line == 0) | (line == L - 1)
+    low = jnp.logical_not(at_end) & (line < L // 2)
 
     def across(n):
-        w = jnp.where(n < L - EARLY, 1, 0)
-        return w, me.order(L - 1 - n + (1 - w) * (L - EARLY))
+        both = 2 * (L - EARLY)
+        n = jnp.where(low & (n == both - 1), both, jnp.where(low & (n == both), both - 1, n))
+        w = jnp.where(n < both, 1 - n % 2, 0)
+        return w, me.order(jnp.where(n < both, L - 1 - n // 2, EARLY - 1 - (n - both)))
+
+    def along(n):
+        t = n - (2 * far - 4)
+        last_low = 2 * far - 4 + jnp.where(t % 2 == 0, 2 + t // 2, t // 2)
+        last_high = 2 * far - 4 + (t % 2) * 2 + t // 2
+        inner = jnp.where(t < 0, n, jnp.where(low, last_low, last_high))
+        outer = jnp.where(n == 0, 2 * far - 2, jnp.where(n == 2 * far - 1, n, n - 1))
+        q = jnp.where(at_end, outer, inner)
+        own = n >= 2 * far
+        return jnp.where(own, 1 - (n - 2 * far), 1 - q % 2), jnp.where(own, 0, L - 1 - q // 2)
+
+    def line_partial(n):
+        w, i = along(n)
+        partial(w, me.order(i) * 2 + side)
+
+    def line_finish(n):
+        w, i = along(n)
+        l = me.order(i)
+        j = l * 2 + side
+        core_copy(w, j).wait_recv()
+
+        @pl.when((w == 0) | (i >= EARLY))
+        def _():
+            remote(
+                from_side.at[w, l], from_side.at[w, l], s_send.at[w, l], s_recv.at[w, l],
+                me.at(line, 1 - side, core),
+            ).wait_recv()
+
+        acc[...] = G[w, j, mine, :].astype(F32) + from_core[w, j].astype(F32) + from_side[w, l].astype(F32)
+
+        @pl.when((l >= line) & (line > 0))
+        def _():
+            remote(
+                from_left.at[w, l], from_left.at[w, l], z_send.at[w, l], l_recv.at[w, l],
+                me.at(line - 1, side, core),
+            ).wait_recv()
+            acc[...] += from_left[w, l].astype(F32)
+
+        @pl.when((l <= line) & (line < L - 1))
+        def _():
+            remote(
+                from_right.at[w, l], from_right.at[w, l], z_send.at[w, l], r_recv.at[w, l],
+                me.at(line + 1, side, core),
+            ).wait_recv()
+            acc[...] += from_right[w, l].astype(F32)
+
+        @pl.when(l == line)
+        def _():
+            for tile in range(H // LANES):
+                rows = pl.ds(tile * 2 + w, R, stride=2 * H // LANES)
+                grad[rows, :] = acc[:, tile * LANES : (tile + 1) * LANES]
+
+        @pl.when(l != line)
+        def _():
+            G[w, j, mine, :] = acc[...].astype(BF16)
+
+        @pl.when(l > line)
+        def _():
+            right_copy(w, l).start()
+
+        @pl.when(l < line)
+        def _():
+            left_copy(w, l).start()
+
+    @pl.when(at_end)
+    def _():
+        line_partial(0)
 
     @pl.loop(0, there + 1)
     def _(n):
-        @pl.when(n == L - EARLY)
+        @pl.when(n == 1)
         def _():
             loads[3].wait()
             loads[4].wait()
@@ -677,17 +752,17 @@
             G[w, j, mine, :] = both.astype(BF16)
             side_copy(w, l).start()
 
-    for c in loads[5:]:
-        c.wait()
-
-    far = L - 1
-
-    def along(n):
-        w, at = 1 - n // far, n % far
-        at_end = (w == 1) & ((line == 0) | (line == L - 1))
-        i = jnp.where(at_end, jnp.where(at == 0, 1, L - at), L - 1 - at)
-        own = n >= 2 * far
-        return jnp.where(own, 1 - (n - 2 * far), w), jnp.where(own, 0, i)
+        @pl.when(n == 2)
+        def _():
+            for c in loads[7:]:
+                c.wait()
+
+        @pl.when((n == 2) & at_end)
+        def _():
+            line_finish(0)
+
+    loads[5].wait()
+    loads[6].wait()
 
     heads_here = FB * wide // HEAD_DIM
     per = wide // HEAD_DIM
@@ -739,12 +814,9 @@
 
     each = -(-heads_here // 2)
 
-    @pl.loop(0, 2 * L)
+    @pl.loop(jnp.where(at_end, 1, 0), 2 * L)
     def _(n):
-        w, i = along(n)
-        l = me.order(i)
-        j = l * 2 + side
-        partial(w, j)
+        line_partial(n)
 
         @pl.when(n == far)
         def _():
@@ -754,48 +826,7 @@
         def _(k):
             attend(k)
 
-        core_copy(w, j).wait_recv()
-
-        @pl.when((w == 0) | (i >= EARLY))
-        def _():
-            remote(
-                from_side.at[w, l], from_side.at[w, l], s_send.at[w, l], s_recv.at[w, l],
-                me.at(line, 1 - side, core),
-            ).wait_recv()
-
-        acc[...] = G[w, j, mine, :].astype(F32) + from_core[w, j].astype(F32) + from_side[w, l].astype(F32)
-
-        @pl.when((l >= line) & (line > 0))
-        def _():
-            remote(
-                from_left.at[w, l], from_left.at[w, l], z_send.at[w, l], l_recv.at[w, l],
-                me.at(line - 1, side, core),
-            ).wait_recv()
-            acc[...] += from_left[w, l].astype(F32)
-
-        @pl.when((l <= line) & (line < L - 1))
-        def _():
-            remote(
-                from_right.at[w, l], from_right.at[w, l], z_send.at[w, l], r_recv.at[w, l],
-                me.at(line + 1, side, core),
-            ).wait_recv()
-            acc[...] += from_right[w, l].astype(F32)
-
-        @pl.when(l == line)
-        def _():
-            grad[w] = acc[...]
-
-        @pl.when(l != line)
-        def _():
-            G[w, j, mine, :] = acc[...].astype(BF16)
-
-        @pl.when(l > line)
-        def _():
-            right_copy(w, l).start()
-
-        @pl.when(l < line)
-        def _():
-            left_copy(w, l).start()
+        line_finish(n)
 
     @pl.loop(0, FB)
     def _(b):
@@ -832,7 +863,7 @@
     dma = pltpu.SemaphoreType.DMA
     return pl.pallas_call(
         functools.partial(backward_kernel, n_seq, n_head),
-        out_shape=(S((2, R, H), F32), S((count, FB * wide), BF16)),
+        out_shape=(S((R * 2 * H // LANES, LANES), F32), S((count, FB * wide), BF16)),
         in_specs=[anywhere] * 6 + [vmem],
         out_specs=(vmem, vmem),
         scratch_shapes=[
@@ -876,31 +907,23 @@
 
 
 def update_kernel(decay, share, grad, memory, momentum, memory_out, momentum_out):
-    _, rows, H = grad.shape
-    each = 2 * H // LANES
-    for k in range(2):
-        for tile in range(H // LANES):
-            at = pl.ds(tile * 2 + k, rows, stride=each)
-            new = decay[0] * momentum[at, :] - grad[k, :, tile * LANES : (tile + 1) * LANES]
-            momentum_out[at, :] = new
-            memory_out[at, :] = (1.0 - share[0]) * memory[at, :] + new
+    new = decay[0] * momentum[...] - grad[...]
+    momentum_out[...] = new
+    memory_out[...] = (1.0 - share[0]) * memory[...] + new
 
 
 def update(decay, share, grad, memory, momentum):
-    _, R, H = grad.shape
-    step = R // 4
-    each = 2 * H // LANES
+    rows = grad.shape[0]
     smem = pl.BlockSpec(memory_space=pltpu.SMEM)
-    flat = pl.BlockSpec((step * each, LANES), lambda i: (i, 0))
-    out = jax.ShapeDtypeStruct((R * each, LANES), F32)
-    new_memory, new_momentum = pl.pallas_call(
+    flat = pl.BlockSpec((rows // UPDATE_STEPS, LANES), lambda i: (i, 0))
+    out = jax.ShapeDtypeStruct(grad.shape, F32)
+    return pl.pallas_call(
         update_kernel,
-        grid=(4,),
+        grid=(UPDATE_STEPS,),
         out_shape=(out, out),
-        in_specs=[smem, smem, pl.BlockSpec((2, step, H), lambda i: (0, i, 0)), flat, flat],
+        in_specs=[smem, smem, flat, flat, flat],
         out_specs=(flat, flat),
-    )(decay, share, grad, interleave(memory), interleave(momentum))
-    return layered(new_memory, R, H), layered(new_momentum, R, H)
+    )(decay, share, grad, memory, momentum)
 
 
 def on_device(
@@ -916,7 +939,8 @@
         tokens[0], qkv, memory_tiles, rate_weight[None], forget_rate, R, H, n_seq, n_head, lr_scale
     )
     grad, attended = backward(xx, yy, query, values, recall, early, persistent, n_seq, n_head, R)
-    memory, momentum = update(momentum_decay, forget_share, grad, memory, momentum)
+    memory, momentum = update(momentum_decay, forget_share, grad, memory_tiles, interleave(momentum))
+    memory, momentum = layered(memory, R, H), layered(momentum, R, H)
     return (attended[None], memory, momentum)
 
 

time: 232 us -> 222 us (0.957)
  Pallas kernels: 228 us -> 216 us
    pallas_call x1, Pallas kernels: 93.4 us -> 85.5 us  [backward(): pl.pallas_call(functools.partial(backward_kernel, n_seq, n_head), out_sha...]
    pallas_call x1, Pallas kernels: 8.16 us -> 4.39 us  [update(): pl.pallas_call(update_kernel, grid=(UPDATE_STEPS,), out_shape=(out, out),...]
where the time goes in v2:
time: 222 us; the launch traced here: 219 us
  Pallas kernels  216 us (97%)
    pallas_call x1, Pallas kernels, forward(): pl.pallas_call(functools.partial(forward_kernel, n_seq, n_head, lr_scale)...  126 us
    pallas_call x1, Pallas kernels, backward(): pl.pallas_call(functools.partial(backward_kernel, n_seq, n_head), out_sha...  85.5 us

profile of v2, /device:TPU:11, one launch (start us, length us, event | category | flops | bytes accessed | tf_op | source)
XLA Modules:
  0.0 218.9 jit_solution(16418399921572969737)
XLA Ops:
  0.6 126.1 %shard_map.112 = (bf16[2,8,512,256]{3,2,1,0:T(8,128)(2,1)}, bf16[2,512,2048]{2,1,0:T(8,128)(2,1)}, bf16[4,512,256]{2,1,0:T(8,128)(2,1)}, bf16[4,512,256]{2,1,0:T...) custom-call(bf16[512,2048]{1,0:T(8,128)(2,1)} %bitcast.28, bf16[3,2048,1024]{2,1,0:T(8,128)(2,1)} %bitcast.24, ...), custom_call_target="tpu_custom_call" | custom-call | tf_op jit(solution)/shard_map/pallas_call | solution.py:513
  126.7 85.5 %shard_map.113 = (f32[4096,128]{1,0:T(8,128)}, bf16[512,1024]{1,0:T(8,128)(2,1)}) custom-call(bf16[2,8,512,256]{3,2,1,0:T(8,128)(2,1)} %get-tuple-element.13.xx_in, bf16[2,512,2048]{2,1,0:T(8,128)(2,1)} %get-tuple-element.14.yy_in, bf16[4,512,256]{2,1,0:T(8,128)(2,1)} %get-tuple-element.15.q_in, bf16[4,512,256]{2,1,0:T(8,128)(2,1)} %get-tuple-element.16.v_in, ...), custom_call_target="tpu_custom_call" | custom-call | tf_op jit(solution)/shard_map/pallas_call | solution.py:864
  213.5 0.0 copy-start
  213.5 4.4 %shard_map.114 = (f32[4096,128]{1,0:T(8,128)}, f32[4096,128]{1,0:T(8,128)}) custom-call(f32[1]{0:T(128)S(6)} %copy.17.decay, f32[1]{0:T(128)S(6)} %copy.18.share, f32[4096,128]{1,0:T(8,128)} %get-tuple-element.20.grad, f32[4096,128]{1,0:T(8,128)} %bitcast.26, f32[4096,128]{1,0:T(8,128)} %bitcast.27), custom_call_target="tpu_custom_call" | custom-call | tf_op jit(solution)/shard_map/pallas_call | solution.py:920
  217.9 0.0 copy-done
  217.9 1.0 copy.19
Async XLA Ops:
  213.5 4.4 %copy-start = (bf16[512,1024]{1,0:T(8,128)(2,1)S(1)}, bf16[512,1024]{1,0:T(8,128)(2,1)}, u32[]{:S(2)}) copy-start(bf16[512,1024]{1,0:T(8,128)(2,1)} %get-tuple-element.19) | copy-start | bytes 3145732

commit v3 on v2

--- a/solution.py
+++ b/solution.py
@@ -72,10 +72,10 @@
 
 def forward_kernel(
     n_seq, n_head, lr_scale,
-    tok, qkv, memory, rate_w, forget,
+    tok_in, qkv, memory, rate_w, forget,
     xx_out, yy_out, q_out, v_out, recall_out, g_out,
-    staged, own, W, wbuf, keys, query, values, zk, zz, hk, hq, wh, errs, recall, weight, frb, G, from_core, from_side,
-    w_send, w_recv, f_send, f_recv, k_send, k_recv, e_send, e_recv, qkv_sem, out_sem, block_sem, g_send, g_recv, mem_sem,
+    tok, staged, own, W, wbuf, keys, query, values, zk, zz, hk, hq, wh, errs, recall, weight, frb, G, from_core, from_side,
+    w_send, w_recv, f_send, f_recv, k_send, k_recv, e_send, e_recv, qkv_sem, out_sem, block_sem, g_send, g_recv, mem_sem, tok_sem,
 ):
     me = Place(n_seq, n_head)
     L, line, side, core, head = me.length, me.line, me.side, me.core, me.head
@@ -89,7 +89,9 @@
 
     memory_load = pltpu.make_async_copy(memory, staged, mem_sem)
     memory_load.start()
+    tok_load = pltpu.make_async_copy(tok_in, tok, tok_sem)
     loads = [pltpu.make_async_copy(qkv.at[k], wbuf.at[s], qkv_sem.at[k]) for k, s in ((1, 0), (0, 1), (2, 0))]
+    tok_load.start()
     loads[0].start()
     loads[1].start()
 
@@ -394,6 +396,7 @@
 
         @pl.when(k == 0)
         def _():
+            tok_load.wait()
             project_shared(0, keys, 0)
             loads[2].start()
 
@@ -465,11 +468,6 @@
     rows_loop(count, 16, pull)
     wdz_out = pltpu.make_async_copy(hk, yy_out.at[0], out_sem.at[4])
     wdz_out.start()
-    early_out = []
-    for i in range(EARLY):
-        early_side(i).wait_recv()
-        early_out.append(pltpu.make_async_copy(from_side.at[i], g_out.at[i], out_sem.at[5 + i]))
-        early_out[i].start()
 
     for c in fcopies:
         c.wait_send()
@@ -487,14 +485,19 @@
                 spread(w, l, p, lambda c: c.wait_send())
                 copy(w, l, 1 - side, core, p, 3).wait_send()
 
-    for i in range(EARLY):
-        early_core(i).wait_send()
-        early_side(i).wait_send()
-
     @pl.loop(0, chips)
     def _(j):
         err_copy(j).wait()
         recall_copy(j).wait()
+
+    early_out = []
+    for i in range(EARLY):
+        early_side(i).wait_recv()
+        early_out.append(pltpu.make_async_copy(from_side.at[i], g_out.at[i], out_sem.at[5 + i]))
+        early_out[i].start()
+    for i in range(EARLY):
+        early_core(i).wait_send()
+        early_side(i).wait_send()
 
     for c in (keys_out, values_out, query_out, wh_out, wdz_out, *early_out):
         c.wait()
@@ -520,9 +523,10 @@
             S((chips, count, wide), BF16),
             S((EARLY, R, H), BF16),
         ),
-        in_specs=[vmem, anywhere, anywhere, vmem, vmem],
+        in_specs=[anywhere, anywhere, anywhere, vmem, vmem],
         out_specs=(anywhere,) * 6,
         scratch_shapes=[
+            pltpu.VMEM(tok.shape, BF16),
             pltpu.VMEM(memory.shape, F32),
             pltpu.VMEM((2, R, H), BF16),
             pltpu.VMEM((2, chips, wide, H), BF16),
@@ -556,6 +560,7 @@
             dma((2, EARLY)),
             dma((2, EARLY)),
             dma,
+            dma,
         ],
         compiler_params=pltpu.CompilerParams(
             collective_id=0, has_side_effects=True, vmem_limit_bytes=VMEM_LIMIT
@@ -565,9 +570,9 @@
 
 def backward_kernel(
     n_seq, n_head,
-    xx_in, yy_in, q_in, v_in, recall_in, g_in, persist,
+    xx_in, yy_in, q_in, v_in, recall_in, g_in, persist_in,
     grad, attended,
-    xx, yy, query, values, recall, got, recalled, G, from_core, from_side, from_left, from_right, acc,
+    persist, xx, yy, query, values, recall, got, recalled, G, from_core, from_side, from_left, from_right, acc,
     c_send, c_recv, s_send, s_recv, z_send, l_recv, r_recv, x_send, x_recv, in_sem,
 ):
     me = Place(n_seq, n_head)
@@ -580,7 +585,7 @@
 
     pairs = (
         (recall_in, recall), (xx_in.at[1], xx.at[1]), (yy_in.at[1], yy.at[1]), (xx_in.at[0], xx.at[0]),
-        (yy_in.at[0], yy.at[0]), (q_in, query), (v_in, values),
+        (yy_in.at[0], yy.at[0]), (q_in, query), (v_in, values), (persist_in, persist),
         *[(g_in.at[i], from_side.at[1, me.order(i)]) for i in range(EARLY)],
     )
     loads = [pltpu.make_async_copy(a, b, in_sem.at[i]) for i, (a, b) in enumerate(pairs)]
@@ -754,15 +759,15 @@
 
         @pl.when(n == 2)
         def _():
-            for c in loads[7:]:
+            for c in loads[8:]:
                 c.wait()
 
         @pl.when((n == 2) & at_end)
         def _():
             line_finish(0)
 
-    loads[5].wait()
-    loads[6].wait()
+    for c in loads[5:8]:
+        c.wait()
 
     heads_here = FB * wide // HEAD_DIM
     per = wide // HEAD_DIM
@@ -814,10 +819,26 @@
 
     each = -(-heads_here // 2)
 
+    def sent():
+        @pl.loop(0, FB)
+        def _(b):
+            for p in range(n_head - 1):
+                rcopy(b, p).wait_send()
+
+        @pl.loop(0, there)
+        def _(n):
+            w, l = across(n)
+            core_copy(w, l * 2 + 1 - side).wait_send()
+            side_copy(w, l).wait_send()
+
     @pl.loop(jnp.where(at_end, 1, 0), 2 * L)
     def _(n):
         line_partial(n)
 
+        @pl.when(n == 2 * L - 1)
+        def _():
+            sent()
+
         @pl.when(n == far)
         def _():
             recall_all()
@@ -827,17 +848,6 @@
             attend(k)
 
         line_finish(n)
-
-    @pl.loop(0, FB)
-    def _(b):
-        for p in range(n_head - 1):
-            rcopy(b, p).wait_send()
-
-    @pl.loop(0, there)
-    def _(n):
-        w, l = across(n)
-        core_copy(w, l * 2 + 1 - side).wait_send()
-        side_copy(w, l).wait_send()
 
     @pl.loop(0, L)
     def _(l):
@@ -864,9 +874,10 @@
     return pl.pallas_call(
         functools.partial(backward_kernel, n_seq, n_head),
         out_shape=(S((R * 2 * H // LANES, LANES), F32), S((count, FB * wide), BF16)),
-        in_specs=[anywhere] * 6 + [vmem],
+        in_specs=[anywhere] * 7,
         out_specs=(vmem, vmem),
         scratch_shapes=[
+            pltpu.VMEM(persist.shape, BF16),
             pltpu.VMEM((2, chips, count, wide), BF16),
             pltpu.VMEM((2, count, H), BF16),
             pltpu.VMEM((FB, count, wide), BF16),
@@ -889,7 +900,7 @@
             dma((2, L)),
             dma((max(n_head - 1, 1), FB)),
             dma((n_head, FB)),
-            dma((7 + EARLY,)),
+            dma((8 + EARLY,)),
         ],
         compiler_params=pltpu.CompilerParams(
             collective_id=1, has_side_effects=True, vmem_limit_bytes=VMEM_LIMIT

time: 222 us -> 220 us (level)
  no operation moved by 1% of the time
where the time goes in v3:
time: 220 us; the launch traced here: 217 us
  Pallas kernels  214 us (97%)
    pallas_call x1, Pallas kernels, forward(): pl.pallas_call(functools.partial(forward_kernel, n_seq, n_head, lr_scale)...  125 us
    pallas_call x1, Pallas kernels, backward(): pl.pallas_call(functools.partial(backward_kernel, n_seq, n_head), out_sha...  84.3 us

profile of v3, /device:TPU:11, one launch (start us, length us, event | category | flops | bytes accessed | tf_op | source)
XLA Modules:
  0.0 216.8 jit_solution(10521347763341455475)
XLA Ops:
  0.6 125.2 %shard_map.112 = (bf16[2,8,512,256]{3,2,1,0:T(8,128)(2,1)}, bf16[2,512,2048]{2,1,0:T(8,128)(2,1)}, bf16[4,512,256]{2,1,0:T(8,128)(2,1)}, bf16[4,512,256]{2,1,0:T...) custom-call(bf16[512,2048]{1,0:T(8,128)(2,1)} %bitcast.28, bf16[3,2048,1024]{2,1,0:T(8,128)(2,1)} %bitcast.24, ...), custom_call_target="tpu_custom_call" | custom-call | tf_op jit(solution)/shard_map/pallas_call | solution.py:516
  125.8 84.3 %shard_map.113 = (f32[4096,128]{1,0:T(8,128)}, bf16[512,1024]{1,0:T(8,128)(2,1)}) custom-call(bf16[2,8,512,256]{3,2,1,0:T(8,128)(2,1)} %get-tuple-element.13.xx_in, bf16[2,512,2048]{2,1,0:T(8,128)(2,1)} %get-tuple-element.14.yy_in, bf16[4,512,256]{2,1,0:T(8,128)(2,1)} %get-tuple-element.15.q_in, bf16[4,512,256]{2,1,0:T(8,128)(2,1)} %get-tuple-element.16.v_in, ...), custom_call_target="tpu_custom_call" | custom-call | tf_op jit(solution)/shard_map/pallas_call | solution.py:874
  211.4 0.0 copy-start
  211.4 4.4 %shard_map.114 = (f32[4096,128]{1,0:T(8,128)}, f32[4096,128]{1,0:T(8,128)}) custom-call(f32[1]{0:T(128)S(6)} %copy.17.decay, f32[1]{0:T(128)S(6)} %copy.18.share, f32[4096,128]{1,0:T(8,128)} %get-tuple-element.20.grad, f32[4096,128]{1,0:T(8,128)} %bitcast.26, f32[4096,128]{1,0:T(8,128)} %bitcast.27), custom_call_target="tpu_custom_call" | custom-call | tf_op jit(solution)/shard_map/pallas_call | solution.py:931
  215.8 0.0 copy-done
  215.8 1.0 copy.19
Async XLA Ops:
  211.4 4.4 %copy-start = (bf16[512,1024]{1,0:T(8,128)(2,1)S(1)}, bf16[512,1024]{1,0:T(8,128)(2,1)}, u32[]{:S(2)}) copy-start(bf16[512,1024]{1,0:T(8,128)(2,1)} %get-tuple-element.19) | copy-start | bytes 3145732

commit v4 on v3

--- a/solution.py
+++ b/solution.py
@@ -589,7 +589,7 @@
         *[(g_in.at[i], from_side.at[1, me.order(i)]) for i in range(EARLY)],
     )
     loads = [pltpu.make_async_copy(a, b, in_sem.at[i]) for i, (a, b) in enumerate(pairs)]
-    for c in (loads[1], loads[2], loads[0], *loads[3:]):
+    for c in loads[1:3]:
         c.start()
 
     barrier = pltpu.get_barrier_semaphore()
@@ -612,17 +612,12 @@
         greet(peer)
     ends = jnp.where(line > 0, 1, 0) + jnp.where(line < L - 1, 1, 0)
     pl.semaphore_wait(barrier, 2 + n_head - 1 + ends)
+    for c in (loads[3], loads[4], loads[0], *loads[5:]):
+        c.start()
 
     def rcopy(b, p):
         there = peers[p]["head"] * FB
         return remote(recall.at[there + b], got.at[head, b], x_send.at[p, b], x_recv.at[head, b], peers[p])
-
-    loads[0].wait()
-
-    @pl.loop(0, FB)
-    def _(b):
-        for p in range(n_head - 1):
-            rcopy(b, p).start()
 
     for c in loads[1:3]:
         c.wait()
@@ -732,10 +727,6 @@
         def _():
             left_copy(w, l).start()
 
-    @pl.when(at_end)
-    def _():
-        line_partial(0)
-
     @pl.loop(0, there + 1)
     def _(n):
         @pl.when(n == 1)
@@ -757,8 +748,19 @@
             G[w, j, mine, :] = both.astype(BF16)
             side_copy(w, l).start()
 
+        @pl.when((n == 1) & at_end)
+        def _():
+            line_partial(0)
+
         @pl.when(n == 2)
         def _():
+            loads[0].wait()
+
+            @pl.loop(0, FB)
+            def _(b):
+                for p in range(n_head - 1):
+                    rcopy(b, p).start()
+
             for c in loads[8:]:
                 c.wait()
 

time: 220 us -> 219 us (level); the launches traced: 217 us -> 218 us
  no operation moved by 1% of the time
where the time goes in v4:
time: 219 us; the launch traced here: 218 us
  Pallas kernels  216 us (99%)
    pallas_call x1, Pallas kernels, forward(): pl.pallas_call(functools.partial(forward_kernel, n_seq, n_head, lr_scale)...  125 us
    pallas_call x1, Pallas kernels, backward(): pl.pallas_call(functools.partial(backward_kernel, n_seq, n_head), out_sha...  86 us
    pallas_call x1, Pallas kernels, update(): pl.pallas_call(update_kernel, grid=(UPDATE_STEPS,), out_shape=(out, out),...  4.39 us

profile of v4, /device:TPU:11, one launch (start us, length us, event | category | flops | bytes accessed | tf_op | source)
XLA Modules:
  0.0 218.5 jit_solution(6066176146239097959)
XLA Ops:
  0.6 125.2 %shard_map.112 = (bf16[2,8,512,256]{3,2,1,0:T(8,128)(2,1)}, bf16[2,512,2048]{2,1,0:T(8,128)(2,1)}, bf16[4,512,256]{2,1,0:T(8,128)(2,1)}, bf16[4,512,256]{2,1,0:T...) custom-call(bf16[512,2048]{1,0:T(8,128)(2,1)} %bitcast.28, bf16[3,2048,1024]{2,1,0:T(8,128)(2,1)} %bitcast.24, ...), custom_call_target="tpu_custom_call" | custom-call | tf_op jit(solution)/shard_map/pallas_call | solution.py:516
  125.8 86.0 %shard_map.113 = (f32[4096,128]{1,0:T(8,128)}, bf16[512,1024]{1,0:T(8,128)(2,1)}) custom-call(bf16[2,8,512,256]{3,2,1,0:T(8,128)(2,1)} %get-tuple-element.13.xx_in, bf16[2,512,2048]{2,1,0:T(8,128)(2,1)} %get-tuple-element.14.yy_in, bf16[4,512,256]{2,1,0:T(8,128)(2,1)} %get-tuple-element.15.q_in, bf16[4,512,256]{2,1,0:T(8,128)(2,1)} %get-tuple-element.16.v_in, ...), custom_call_target="tpu_custom_call" | custom-call | tf_op jit(solution)/shard_map/pallas_call | solution.py:876
  213.1 0.0 copy-start
  213.1 4.4 %shard_map.114 = (f32[4096,128]{1,0:T(8,128)}, f32[4096,128]{1,0:T(8,128)}) custom-call(f32[1]{0:T(128)S(6)} %copy.17.decay, f32[1]{0:T(128)S(6)} %copy.18.share, f32[4096,128]{1,0:T(8,128)} %get-tuple-element.20.grad, f32[4096,128]{1,0:T(8,128)} %bitcast.26, f32[4096,128]{1,0:T(8,128)} %bitcast.27), custom_call_target="tpu_custom_call" | custom-call | tf_op jit(solution)/shard_map/pallas_call | solution.py:933
  217.5 0.0 copy-done
  217.5 1.0 copy.19
Async XLA Ops:
  213.1 4.4 %copy-start = (bf16[512,1024]{1,0:T(8,128)(2,1)S(1)}, bf16[512,1024]{1,0:T(8,128)(2,1)}, u32[]{:S(2)}) copy-start(bf16[512,1024]{1,0:T(8,128)(2,1)} %get-tuple-element.19) | copy-start | bytes 3145732
